TPU v7x, 32 devices: a whole 2x2x4 slice. The times are simulated.
32 devices in a mesh: section: 4 (over z), fsdp: 4 (over y, core), tp: 2 (over x).
Axes of the slice: x: 2, y: 2, z: 4, core: 2. Of those that a mesh axis runs over, the one named last changes fastest.
Arguments:
- stash: bfloat16 [4, 4, 512, 2304], P('section', None, 'fsdp'), may hold values from -6 to 6
- grad_now: bfloat16 [4, 512, 2304], P('section', 'fsdp'), may hold values from -6 to 6
- grad_top: bfloat16 [2, 512, 2304], P(None, 'fsdp'), may hold values from -6 to 6
- order: int32 [4, 4], P('section'), may hold values from 0 to 3, each once within a row
- gain: float32 [4, 2304], P('section'), may hold values from 0.5 to 1.5
- weight: bfloat16 [4, 2304, 2048], P('section', 'fsdp', 'tp'), may hold values from -0.125 to 0.125
Outputs:
- grad_held: bfloat16 [4, 512, 2304], P('section', 'fsdp')
- weight_grad: float32 [4, 2304, 2048], P('section', 'fsdp', 'tp')
Inputs may be any that keep to these rules, and one draw needn't show every extreme that they name: Each row of order names every kept micro-batch once.
All inputs are finite; a program needn't handle non-finite values.
Results may differ from a plain program's by a relative error of at most 0.013.
Values may be sent and summed in bfloat16 or wider, within the bound.
A program may use at most 64 MiB of HBM per device.

v0:
```python
import jax
import jax.numpy as jnp
from jax import lax
from jax.sharding import PartitionSpec as P

norm_eps = 1e-06


def shifted(shard, axis, by):
    length = lax.axis_size(axis)
    pairs = [(i, i + by) for i in range(length) if 0 <= i + by < length]
    return lax.ppermute(shard, axis, pairs)


def gelu_tanh(values):
    return jax.nn.gelu(values, approximate=True)


def per_device(stash, grad_now, grad_top, order, gain, weight):
    full_weight = lax.all_gather(weight[0], "fsdp", axis=0, tiled=True)
    section_gain = gain[0]
    is_last = lax.axis_index("section") == lax.axis_size("section") - 1
    tp_count = lax.axis_size("tp")
    tp_place = lax.axis_index("tp")
    feature_count = stash.shape[-1]
    share_width = feature_count // tp_count
    share_start = tp_place * share_width
    rows_here = grad_now.shape[1]
    grad_in = grad_now[0]
    lhs_parts = []
    rhs_parts = []
    for tick_id in range(grad_top.shape[0]):
        slot_id = order[0, tick_id]
        section_in = lax.dynamic_index_in_dim(stash[0], slot_id, 0, keepdims=False)
        values = section_in.astype(jnp.float32)
        inv_rms = lax.rsqrt(jnp.mean(values * values, axis=-1, keepdims=True) + norm_eps)
        scaled = values * inv_rms
        normed = (scaled * section_gain).astype(jnp.bfloat16)
        stacked = jnp.concatenate([normed, grad_in], axis=0)
        products = jnp.dot(stacked, full_weight, preferred_element_type=jnp.float32)
        hidden = products[:rows_here]
        backed = products[rows_here:]
        activated, pullback = jax.vjp(gelu_tanh, hidden)
        grad_pre = pullback(backed)[0].astype(jnp.bfloat16)
        activated = activated.astype(jnp.bfloat16)
        lhs_parts.append(normed)
        lhs_parts.append(grad_in)
        rhs_parts.append(grad_pre)
        rhs_parts.append(activated)
        partial_dh = lax.dot_general(
            grad_pre, full_weight, (((1,), (1,)), ((), ())), preferred_element_type=jnp.float32
        )
        total_share = lax.psum_scatter(
            partial_dh.astype(jnp.bfloat16), "tp", scatter_dimension=1, tiled=True
        ).astype(jnp.float32)
        scaled_share = lax.dynamic_slice_in_dim(scaled, share_start, share_width, 1)
        gain_share = lax.dynamic_slice_in_dim(section_gain, share_start, share_width, 0)
        grad_share = lax.dynamic_slice_in_dim(grad_in, share_start, share_width, 1)
        gained = gain_share * total_share
        moment_sum = lax.psum(jnp.sum(gained * scaled_share, axis=-1), "tp")
        inner_mean = (moment_sum / feature_count)[:, None]
        out_share = (
            grad_share.astype(jnp.float32) + inv_rms * (gained - scaled_share * inner_mean)
        ).astype(jnp.bfloat16)
        arrived = shifted(out_share, "section", -1)
        top_share = lax.dynamic_slice_in_dim(grad_top[tick_id], share_start, share_width, 1)
        held_share = jnp.where(is_last, top_share, arrived)
        grad_in = lax.all_gather(held_share, "tp", axis=1, tiled=True)
    lhs_all = jnp.concatenate(lhs_parts, axis=0)
    rhs_all = jnp.concatenate(rhs_parts, axis=0)
    weight_grad = lax.psum_scatter(
        lax.dot_general(
            lhs_all, rhs_all, (((0,), (0,)), ((), ())), preferred_element_type=jnp.float32
        ).astype(jnp.bfloat16),
        "fsdp",
        scatter_dimension=0,
        tiled=True,
    ).astype(jnp.float32)
    return (grad_in[None], weight_grad[None])


def solution(mesh):
    return jax.shard_map(
        per_device,
        mesh=mesh,
        in_specs=(
            P("section", None, "fsdp", None),
            P("section", "fsdp", None),
            P(None, "fsdp", None),
            P("section", None),
            P("section", None),
            P("section", "fsdp", "tp"),
        ),
        out_specs=(P("section", "fsdp", None), P("section", "fsdp", "tp")),
        check_vma=False,
    )
```

profile of v0, /device:TPU:0, one launch (start us, length us, event | category | flops | bytes accessed | tf_op | source)
XLA Modules:
  0.0 181.7 jit_solution(16638024135752744247)
XLA Ops:
  7.9 1.3 fusion.55
  13.9 1.6 fusion.22
  15.5 2.3 %multiply_convert_fusion = (bf16[128,2304]{1,0:T(8,128)(2,1)}, bf16[128,2304]{1,0:T(8,128)(2,1)S(1)}, f32[128,2304]{1,0:T(8,128)S(1)}, f32[128,2304]{1,0:T(8,128)S(1)}) fusion(f32[2304]{0:T(1024)S(1)} %reduce.1, f32[128]{0:T(128)S(1)} %get-tuple-element.16, bf16[1,4,128,2304]{3,2,1,0:T(8,128)(2,1)} %param.6, s32[]{:T(128)S(6)} %select_n.33, ...), kind=kLoop, calls=%fused_computation.31 | loop fusion | flops 2359296 | bytes 4728840 | tf_op jit(solution)/shard_map/convert_element_type | solution.py:38
  17.7 32.0 %all-gather.3.cloned.1.call-done = bf16[1,2304,1024]{2,1,0:T(8,128)(2,1)} async-done(((bf16[1,576,1024]{2,1,0:T(8,128)(2,1)}), bf16[1,2304,1024]{2,1,0:T(8,128)(2,1)}) %all-gather.3.cloned.1.call-update) | async-done | bytes 4718608 | tf_op jit(solution)/shard_map/all_gather | solution.py:20
  49.7 4.0 %fusion.6 = f32[256,1024]{1,0:T(8,128)S(1)} fusion(bf16[1,2304,1024]{2,1,0:T(8,128)(2,1)} %all-gather.3.cloned.1.call-done, bf16[128,2304]{1,0:T(8,128)(2,1)} %bitcast.52, bf16[128,2304]{1,0:T(8,128)(2,1)S(1)} %get-tuple-element.5), kind=kOutput, calls=%fused_computation.7 | convolution fusion | flops 1210318848 | bytes 6946816 | tf_op jit(solution)/shard_map/dot_general | solution.py:40
  54.9 1.7 fusion.8
  57.7 15.4 %reduce-scatter.10.cloned.1.call-done = bf16[1152,128]{1,0:T(8,128)(2,1)} async-done(((bf16[2304,128]{1,0:T(8,128)(2,1)}), bf16[1152,128]{1,0:T(8,128)(2,1)}) %reduce-scatter.10.cloned.1.call-update) | async-done | bytes 294928
  73.1 1.2 copy.9
  74.5 4.9 %psum.14 = f32[128]{0:T(128)S(1)} all-reduce(f32[128]{0:T(128)S(1)} %multiply_reduce_fusion.1), channel_id=1, replica_groups=mesh['section'=4,'fsdp'=4,'tp'=2] {'tp'}, use_global_device_ids=true, to_apply=%region_3.4 | all-reduce | flops 128 | bytes 1024 | tf_op jit(solution)/shard_map/psum | solution.py:60
  79.4 1.3 fusion.36
  80.7 1.4 collective-permute-start
  82.2 8.0 %collective-permute-done = bf16[128,1152]{1,0:T(8,128)(2,1)} collective-permute-done((bf16[128,1152]{1,0:T(8,128)(2,1)S(1)}, bf16[128,1152]{1,0:T(8,128)(2,1)}, u32[]{:S(2)}, u32[]{:S(2)}) %collective-permute-start) | collective-permute-done | bytes 294944 | tf_op jit(solution)/shard_map/ppermute | solution.py:12
  91.3 7.5 %all_gather.10 = bf16[128,2304]{1,0:T(8,128)(2,1)S(1)} all-gather(bf16[128,1152]{1,0:T(8,128)(2,1)S(1)} %bitcast_select_fusion), channel_id=1, replica_groups=mesh['section'=4,'fsdp'=4,'tp'=2] {'tp'}, dimensions={1}, use_global_device_ids=true | all-gather | bytes 884736 | tf_op jit(solution)/shard_map/all_gather | solution.py:68
  98.8 3.8 %fusion.2 = f32[256,1024]{1,0:T(8,128)S(1)} fusion(bf16[1,2304,1024]{2,1,0:T(8,128)(2,1)} %all-gather.3.cloned.1.call-done, bf16[128,2304]{1,0:T(8,128)(2,1)S(1)} %all_gather.10, bf16[128,2304]{1,0:T(8,128)(2,1)S(1)} %copy-done.2), kind=kOutput, calls=%fused_computation.3 | convolution fusion | flops 1210318848 | bytes 6946816 | tf_op jit(solution)/shard_map/dot_general | solution.py:40
  103.7 1.7 fusion.11
  106.5 6.3 %convolution_convert_fusion = bf16[2304,1024]{1,0:T(8,128)(2,1)} fusion(bf16[128,2304]{1,0:T(8,128)(2,1)S(1)} %all_gather.10, bf16[128,2304]{1,0:T(8,128)(2,1)} %get-tuple-element.4, bf16[128,2304]{1,0:T(8,128)(2,1)} %bitcast.53, bf16[128,2304]{1,0:T(8,128)(2,1)} %copy-done.3, bf16[128,1024]{1,0:T(8,128)(2,1)} %get-tuple-element.12, ...), kind=kOutput, calls=%fused_computation | convolution fusion | flops 2431909888 | bytes 8126464 | tf_op jit(solution)/shard_map/dot_general | solution.py:72
  112.8 8.2 %reduce-scatter.12.cloned.1.call-done = bf16[1152,128]{1,0:T(8,128)(2,1)} async-done(((bf16[2304,128]{1,0:T(8,128)(2,1)}), bf16[1152,128]{1,0:T(8,128)(2,1)}) %reduce-scatter.12.cloned.1.call-update) | async-done | bytes 294928
  121.0 1.2 copy.11
  122.3 4.9 %psum.15 = f32[128]{0:T(128)S(1)} all-reduce(f32[128]{0:T(128)S(1)} %multiply_reduce_fusion), channel_id=1, replica_groups=mesh['section'=4,'fsdp'=4,'tp'=2] {'tp'}, use_global_device_ids=true, to_apply=%region_7.8 | all-reduce | flops 128 | bytes 1024 | tf_op jit(solution)/shard_map/psum | solution.py:60
  127.5 1.3 collective-permute-start.1
  128.8 8.0 %collective-permute-done.1 = bf16[128,1152]{1,0:T(8,128)(2,1)S(1)} collective-permute-done((bf16[128,1152]{1,0:T(8,128)(2,1)S(1)}, bf16[128,1152]{1,0:T(8,128)(2,1)S(1)}, u32[]{:S(2)}, u32[]{:S(2)}) %collective-permute-start.1) | collective-permute-done | bytes 294944 | tf_op jit(solution)/shard_map/ppermute | solution.py:12
  136.9 7.4 %all_gather.11 = bf16[128,2304]{1,0:T(8,128)(2,1)S(1)} all-gather(bf16[128,1152]{1,0:T(8,128)(2,1)S(1)} %bitcast_select_fusion.1), channel_id=1, replica_groups=mesh['section'=4,'fsdp'=4,'tp'=2] {'tp'}, dimensions={1}, use_global_device_ids=true | all-gather | bytes 884736 | tf_op jit(solution)/shard_map/all_gather | solution.py:68
  144.3 27.2 %reduce-scatter.8.cloned.1.call-done = bf16[576,1024]{1,0:T(8,128)(2,1)} async-done(((bf16[2304,1024]{1,0:T(8,128)(2,1)}), bf16[576,1024]{1,0:T(8,128)(2,1)}) %reduce-scatter.8.cloned.1.call-update) | async-done | bytes 1179664 | tf_op jit(solution)/shard_map/reduce_scatter | solution.py:71
  171.4 3.0 %bitcast_convert_fusion = f32[1,576,1024]{2,1,0:T(8,128)} fusion(bf16[576,1024]{1,0:T(8,128)(2,1)} %reduce-scatter.8.cloned.1.call-done), kind=kLoop, calls=%fused_computation.30 | loop fusion | flops 589824 | bytes 3538944 | tf_op jit(solution)/shard_map/broadcast_in_dim | solution.py:79
  (39 shorter events, 8.5 us)
Async XLA Ops:
  7.2 42.6 %all-gather.3.cloned.1.call-start = ((), (), s32[]{:S(2)}) async-start(), calls=%async_computation.4 | async-start | bytes 5898240 | tf_op jit(solution)/shard_map/all_gather | solution.py:20
  7.9 65.2 %reduce-scatter.10.cloned.1.call-start = ((), (), s32[]{:S(2)}) async-start(), calls=%async_computation.5 | async-start | bytes 884736
  17.7 36.1 %copy-start.3 = (bf16[128,2304]{1,0:T(8,128)(2,1)}, bf16[128,2304]{1,0:T(8,128)(2,1)S(1)}, u32[]{:S(2)}) copy-start(bf16[128,2304]{1,0:T(8,128)(2,1)S(1)} %get-tuple-element.5) | copy-start | bytes 1769476
  49.7 5.1 %copy-start = (bf16[1,2304,1024]{2,1,0:T(8,128)(2,1)S(1)}, bf16[1,2304,1024]{2,1,0:T(8,128)(2,1)}, u32[]{:S(2)}) copy-start(bf16[1,2304,1024]{2,1,0:T(8,128)(2,1)} %all-gather.3.cloned.1.call-done) | copy-start | bytes 14155780
  54.9 2.8 %copy-start.4 = (f32[1,2304]{1,0:T(1,128)S(1)}, f32[1,2304]{1,0:T(1,128)}, u32[]{:S(2)}) copy-start(f32[1,2304]{1,0:T(1,128)} %param.10) | copy-start | bytes 27652
  57.6 63.4 %reduce-scatter.12.cloned.1.call-start = ((), (), s32[]{:S(2)}) async-start(), calls=%async_computation.6 | async-start | bytes 884736
  79.4 2.7 %copy-start.1 = (bf16[2,128,2304]{2,1,0:T(8,128)(2,1)S(1)}, bf16[2,128,2304]{2,1,0:T(8,128)(2,1)}, u32[]{:S(2)}) copy-start(bf16[2,128,2304]{2,1,0:T(8,128)(2,1)} %param.8) | copy-start | bytes 3538948
  80.7 18.1 %copy-start.2 = (bf16[128,2304]{1,0:T(8,128)(2,1)S(1)}, bf16[128,2304]{1,0:T(8,128)(2,1)}, u32[]{:S(2)}) copy-start(bf16[128,2304]{1,0:T(8,128)(2,1)} %get-tuple-element.4) | copy-start | bytes 1769476
  80.7 9.5 %collective-permute-start = (bf16[128,1152]{1,0:T(8,128)(2,1)S(1)}, bf16[128,1152]{1,0:T(8,128)(2,1)}, u32[]{:S(2)}, u32[]{:S(2)}) collective-permute-start(bf16[128,1152]{1,0:T(8,128)(2,1)S(1)} %fusion.36), channel_id=1, source_target_pairs={{8,0},{16,8},{24,16},{9,1},{17,9},{25,17},{10,2},{18,10},{26,18},{... | collective-permute-start | bytes 884744 | tf_op jit(solution)/shard_map/ppermute | solution.py:12
  91.2 12.4 %slice-start = ((s8[4718592]{0:T(1024)(128)(4,1)}), s8[4194304]{0:T(1024)(128)(4,1)S(1)}, s32[]{:S(2)}) async-start(s8[4718592]{0:T(1024)(128)(4,1)} %bitcast.45), calls=%async_computation.7 | async-start | bytes 8388608
  98.8 4.9 %slice-start.1 = ((s8[4718592]{0:T(1024)(128)(4,1)}), s8[524288]{0:T(1024)(128)(4,1)S(1)}, s32[]{:S(2)}) async-start(s8[4718592]{0:T(1024)(128)(4,1)} %bitcast.45), calls=%async_computation.8 | async-start | bytes 1048576
  106.4 65.0 %reduce-scatter.8.cloned.1.call-start = ((), (), s32[]{:S(2)}) async-start(), calls=%async_computation.3 | async-start | bytes 5898240 | tf_op jit(solution)/shard_map/reduce_scatter | solution.py:71
  127.5 9.3 %collective-permute-start.1 = (bf16[128,1152]{1,0:T(8,128)(2,1)S(1)}, bf16[128,1152]{1,0:T(8,128)(2,1)S(1)}, u32[]{:S(2)}, u32[]{:S(2)}) collective-permute-start(bf16[128,1152]{1,0:T(8,128)(2,1)S(1)} %add_convert_fusion), channel_id=1, source_target_pairs={{8,0},{16,8},{24,16},{9,1},{17,9},{25,17},{10,2},{18,10},{26,18},{... | collective-permute-start | bytes 884744 | tf_op jit(solution)/shard_map/ppermute | solution.py:12
Sparse Core Ops, SparseCore 0:
  9.5 40.1 all-gather.2
  57.7 15.3 reduce-scatter.9
  106.5 14.4 reduce-scatter.11
  123.4 47.9 reduce-scatter.7
where the time goes:
time: 182 us
  waiting for transfers between devices  99.5 us (55%)
  blocking collectives  24.8 us (14%)
  between operations  17.8 us (10%)
  matrix products  17.5 us (10%)
  other arithmetic  12.6 us (7%)
  local copies, waits for them, and re-layouts  6.68 us (4%)
  starting transfers between devices  2.88 us (2%)
    all_gather x1, waiting for transfers between devices, per_device(): full_weight = lax.all_gather(weight[0], 'fsdp', axis=0, tiled=True)  32 us
    reduce_scatter x1, waiting for transfers between devices, per_device(): lax.psum_scatter(lax.dot_general(lhs_all, rhs_all, (((0,), (0,)), ((), ()...  27.2 us
    unnamed x6, waiting for transfers between devices  24.3 us
    ppermute x2, waiting for transfers between devices, shifted(): return lax.ppermute(shard, axis, pairs)  16 us
    all_gather x2, blocking collectives, per_device(): grad_in = lax.all_gather(held_share, 'tp', axis=1, tiled=True)  14.9 us
    psum x2, blocking collectives, per_device(): moment_sum = lax.psum(jnp.sum(gained * scaled_share, axis=-1), 'tp')  9.85 us
    dot_general x2, matrix products, per_device(): products = jnp.dot(stacked, full_weight, preferred_element_type=jnp.float32)  7.83 us
    dot_general x1, matrix products, per_device(): lax.dot_general(lhs_all, rhs_all, (((0,), (0,)), ((), ())), preferred_ele...  6.34 us
  transfers between devices with their start and end apart: 6, of which 6 were waited for; matrix products, arithmetic and copies ran while one was open for 8% of the time, Pallas kernels for 0%

commit v1 on v0

v1 whole, which is shorter than its diff:
```python
import functools

import jax
import jax.numpy as jnp
from jax import lax
from jax.experimental import pallas as pl
from jax.experimental.pallas import tpu as pltpu
from jax.sharding import PartitionSpec as P

norm_eps = 1e-06
MESH = pl.DeviceIdType.MESH
f32 = jnp.float32
bf16 = jnp.bfloat16
LAG = 2


def gelu_parts(u):
    k = 0.7978845608028654
    c = 0.044715
    u2 = u * u
    t = jnp.tanh(k * u * (1.0 + c * u2))
    half = 0.5 * (1.0 + t)
    act = u * half
    slope = half + 0.5 * u * (1.0 - t * t) * (k * (1.0 + 3.0 * c * u2))
    return act, slope


def pick(extent, options):
    for o in options:
        if extent % o == 0:
            return o
    return extent


def kernel(
    S, FS, TP, T, order_ref, gain_ref, stash_ref, gnow_ref, gtop_ref, w_ref,
    held_ref, wg_ref,
    wfull, stash, act, xt, inv, dyn, lt, lta, rhs, prod, slope, own_e, peer_e, dxs, acc,
    lsem, topsem, ownsem, heldsem, w_s, w_r, l_s, l_r, r_s, r_r, e_s, e_r, z_s, z_r,
):
    s = lax.axis_index("section")
    f = lax.axis_index("fsdp")
    p = lax.axis_index("tp")
    NC = FS // 2
    yc = f // 2
    core = f % 2
    sib = 2 * yc + (1 - core)
    n, D = act.shape[0] // (T + 1), act.shape[1]
    wl, N = w_ref.shape[1], w_ref.shape[2]
    WCH = w_s.shape[1]
    wc = wl // WCH
    CW = D // e_s.shape[-1]
    CH = D // CW
    nw = pick(N, (256, 128))

    loads = [
        pltpu.make_async_copy(w_ref.at[0], wfull.at[pl.ds(f * wl, wl), :], lsem.at[0]),
        pltpu.make_async_copy(stash_ref.at[0], stash, lsem.at[1]),
        pltpu.make_async_copy(gnow_ref.at[0], act.at[pl.ds(T * n, n), :], lsem.at[2]),
    ]
    for c in loads:
        c.start()

    bar = pltpu.get_barrier_semaphore()
    for r in range(1, FS):
        pl.semaphore_signal(bar, inc=1, device_id={"fsdp": (f + r) % FS}, device_id_type=MESH)
    for r in range(1, TP):
        pl.semaphore_signal(bar, inc=1, device_id={"tp": (p + r) % TP}, device_id_type=MESH)

    @pl.when(s > 0)
    def _():
        pl.semaphore_signal(bar, inc=1, device_id={"section": s - 1}, device_id_type=MESH)

    @pl.when(s < S - 1)
    def _():
        pl.semaphore_signal(bar, inc=1, device_id={"section": s + 1}, device_id_type=MESH)

    pl.semaphore_wait(bar, FS - 1 + TP - 1 + jnp.minimum(s, 1) + jnp.minimum(S - 1 - s, 1))

    def rcopy(src, dst, ss, rs, dev):
        return pltpu.make_async_remote_copy(
            src_ref=src, dst_ref=dst, send_sem=ss, recv_sem=rs, device_id=dev, device_id_type=MESH
        )

    def w_copy(k, j):
        if k < NC:
            rows = pl.ds(f * wl + j * wc, wc)
            src = w_ref.at[0, pl.ds(j * wc, wc), :]
            to = sib if k == 0 else 2 * ((yc + k) % NC) + core
        else:
            o = k - NC + 1
            rows = pl.ds((2 * ((yc - o + NC) % NC) + core) * wl + j * wc, wc)
            src = wfull.at[rows, :]
            to = sib
        return rcopy(src, wfull.at[rows, :], w_s.at[k, j], w_r.at[k, j], {"fsdp": to})

    for k in list(range(1, NC)) + [0]:
        for j in range(WCH):
            w_copy(k, j).start()

    def l_copy(part, r):
        to = (f + r) % FS
        return rcopy(
            lt.at[part, pl.ds(to * wl, wl), :], lta.at[part, :, pl.ds(pl.multiple_of(f * n, n), n)],
            l_s.at[part, r - 1], l_r.at[part, r - 1], {"fsdp": to},
        )

    def l_own(part):
        return pltpu.make_async_copy(
            lt.at[part, pl.ds(f * wl, wl), :], lta.at[part, :, pl.ds(pl.multiple_of(f * n, n), n)],
            ownsem.at[part],
        )

    def l_send(part):
        for r in range(1, FS):
            l_copy(part, r).start()
        l_own(part).start()

    def r_copy(part, k):
        if k < NC:
            at = f
            to = sib if k == 0 else 2 * ((yc + k) % NC) + core
        else:
            o = k - NC + 1
            at = 2 * ((yc - o + NC) % NC) + core
            to = sib
        blk = rhs.at[part, pl.ds(pl.multiple_of(at * n, n), n), :]
        return rcopy(blk, blk, r_s.at[part, k], r_r.at[part, k], {"fsdp": to})

    def r_send(part):
        for k in list(range(1, NC)) + [0]:
            r_copy(part, k).start()

    tw = pick(D, (256, 128))

    def transpose_rows(part, ref, first):
        @pl.loop(0, D // tw)
        def _(i):
            cols = pl.ds(pl.multiple_of(i * tw, tw), tw)
            lt[part, cols, :] = ref[pl.ds(first, n), cols].astype(f32).T.astype(bf16)

    loads[1].wait()
    rb = pick(n, (32, 16))
    for t in range(T):
        slot = order_ref[0, t]

        @pl.loop(0, n // rb)
        def _(i):
            rows = pl.ds(pl.multiple_of(i * rb, rb), rb)
            raw = stash[slot, rows, :]
            v = raw.astype(f32)
            iv = lax.rsqrt(jnp.mean(v * v, axis=-1, keepdims=True) + norm_eps)
            xt[t, rows, :] = raw
            inv[t, rows, :] = jnp.broadcast_to(iv, (rb, 128))
            act[pl.ds(pl.multiple_of(t * n + i * rb, rb), rb), :] = ((v * iv) * gain_ref[0:1, :]).astype(bf16)

        transpose_rows(2 * t, act, t * n)
        if t == 0:
            l_send(0)
            loads[2].wait()
            transpose_rows(1, act, T * n)
            l_send(1)
        else:
            l_send(2 * t)

    @pl.when(s == S - 1)
    def _():
        for t in range(T):
            pltpu.make_async_copy(gtop_ref.at[t], dyn.at[t], topsem.at[t]).start()

    half = 2 * wl

    def part_product(chip, first):
        ks = pl.ds(pl.multiple_of(chip * half, half), half)

        @pl.loop(0, N // nw)
        def _(i):
            cols = pl.ds(pl.multiple_of(i * nw, nw), nw)
            d = jnp.dot(act[:, ks], wfull[ks, cols], preferred_element_type=f32)
            if first:
                prod[:, cols] = d
            else:
                prod[:, cols] += d

    loads[0].wait()
    for j in range(WCH):
        w_copy(0, j).wait_recv()
    part_product(yc, True)
    for o in range(1, NC):
        for j in range(WCH):
            w_copy(o, j).wait_recv()
            w_copy(NC - 1 + o, j).start()
        for j in range(WCH):
            w_copy(NC - 1 + o, j).wait_recv()
        part_product((yc - o + NC) % NC, False)

    mine = pl.multiple_of(f * n, n)

    def gelu_rows(t, with_grad):
        @pl.loop(0, n // rb)
        def _(i):
            rows = pl.ds(pl.multiple_of(t * n + i * rb, rb), rb)
            here = pl.ds(pl.multiple_of(mine + i * rb, rb), rb)
            a, sl = gelu_parts(prod[rows, :])
            rhs[2 * t + 1, here, :] = a.astype(bf16)
            if with_grad:
                g = prod[pl.ds(pl.multiple_of(T * n + i * rb, rb), rb), :]
                rhs[2 * t, here, :] = (sl * g).astype(bf16)
            else:
                slope[t, pl.ds(pl.multiple_of(i * rb, rb), rb), :] = sl

    def e_copy(t, r, c):
        cols = pl.ds(pl.multiple_of(c * CW, CW), CW)
        return rcopy(
            own_e.at[t, :, cols], peer_e.at[t, r - 1, :, cols],
            e_s.at[t, r - 1, c], e_r.at[t, r - 1, c], {"tp": (p + r) % TP},
        )

    def z_copy(t, c):
        cols = pl.ds(pl.multiple_of(c * CW, CW), CW)
        to = jnp.maximum(s - 1, 0)
        return rcopy(
            dxs.at[t, :, cols], dyn.at[t, :, cols], z_s.at[t, c], z_r.at[t, c], {"section": to}
        )

    def spread(t):
        du = rhs[2 * t, pl.ds(mine, n), :]
        u = prod[pl.ds(t * n, n), :]
        m = jnp.sum(du.astype(f32) * u, axis=-1, keepdims=True) / D
        iv = inv[t, :, 0:1]
        q_scale = iv * iv * m

        @pl.loop(0, CH)
        def _(c):
            cols = pl.ds(pl.multiple_of(c * CW, CW), CW)
            dh = lax.dot_general(
                rhs[2 * t, pl.ds(mine, n), :], wfull[cols, :], (((1,), (1,)), ((), ())),
                preferred_element_type=f32,
            )
            e = iv * (gain_ref[0:1, cols] * dh) - xt[t, :, cols].astype(f32) * q_scale
            own_e[t, :, cols] = e.astype(bf16)
            for r in range(1, TP):
                e_copy(t, r, c).start()

    def combine(t, c):
        cols = pl.ds(pl.multiple_of(c * CW, CW), CW)
        for r in range(1, TP):
            e_copy(t, r, c).wait_recv()
        total = own_e[t, :, cols].astype(f32)
        for r in range(1, TP):
            total = total + peer_e[t, r - 1, :, cols].astype(f32)
        dy = act[pl.ds(T * n, n), cols] if t == 0 else dyn[t - 1, :, cols]
        dxs[t, :, cols] = (dy.astype(f32) + total).astype(bf16)
        z_copy(t, c).start()

    for t in range(T):
        if t == 0:
            gelu_rows(0, True)
        r_ids = [0, 1] if t == 0 else [2 * t]

        @pl.when(s > 0)
        def _():
            spread(t)

        for part in r_ids:
            r_send(part)
        if t == 0:
            for later in range(1, T):
                gelu_rows(later, False)
                r_send(2 * later + 1)

        if t < T - 1:
            @pl.when(s == S - 1)
            def _():
                pltpu.make_async_copy(gtop_ref.at[t], dyn.at[t], topsem.at[t]).wait()

            gr = pl.ds(T * n, n)

            @pl.loop(0, CH + LAG)
            def _(i):
                @pl.when((i < CH) & (s > 0))
                def _():
                    combine(t, i)

                @pl.when(i >= LAG)
                def _():
                    c = i - LAG

                    @pl.when(s < S - 1)
                    def _():
                        z_copy(t, c).wait_recv()

                    cols = pl.ds(pl.multiple_of(c * CW, CW), CW)
                    d = dyn[t, :, cols]
                    lt[2 * t + 3, cols, :] = d.astype(f32).T.astype(bf16)
                    g = jnp.dot(d, wfull[cols, :], preferred_element_type=f32)

                    @pl.when(c == 0)
                    def _():
                        prod[gr, :] = g

                    @pl.when(c > 0)
                    def _():
                        prod[gr, :] += g

            l_send(2 * t + 3)

            @pl.loop(0, n // rb)
            def _(i):
                rows = pl.ds(pl.multiple_of(i * rb, rb), rb)
                g = prod[pl.ds(pl.multiple_of(T * n + i * rb, rb), rb), :]
                here = pl.ds(pl.multiple_of(mine + i * rb, rb), rb)
                rhs[2 * t + 2, here, :] = (slope[t + 1, rows, :] * g).astype(bf16)
        else:
            @pl.when(s > 0)
            def _():
                @pl.loop(0, CH)
                def _(c):
                    combine(t, c)

    parts = []
    for t in range(T):
        parts += [2 * t, 2 * t + 1] if t == 0 else [2 * t + 1, 2 * t]
    for at, part in enumerate(parts):
        l_own(part).wait()
        for r in range(1, FS):
            l_copy(part, r).wait_recv()
        for o in range(1, NC):
            r_copy(part, o).wait_recv()
            r_copy(part, NC - 1 + o).start()
        r_copy(part, 0).wait_recv()
        for o in range(1, NC):
            r_copy(part, NC - 1 + o).wait_recv()
        final = at == len(parts) - 1

        @pl.loop(0, N // nw)
        def _(i):
            cols = pl.ds(pl.multiple_of(i * nw, nw), nw)
            d = jnp.dot(lta[part], rhs[part, :, cols], preferred_element_type=f32)
            if at > 0:
                d = acc[:, cols] + d
            if final:
                wg_ref[0, :, cols] = d.astype(bf16)
            else:
                acc[:, cols] = d

    t = T - 1

    @pl.when(s == S - 1)
    def _():
        pltpu.make_async_copy(gtop_ref.at[t], dyn.at[t], topsem.at[t]).wait()

    @pl.when(s < S - 1)
    def _():
        @pl.loop(0, CH)
        def _(c):
            z_copy(t, c).wait_recv()

    out = pltpu.make_async_copy(dyn.at[t], held_ref.at[0], heldsem.at[0])
    out.start()

    for j in range(WCH):
        for k in range(2 * NC - 1):
            w_copy(k, j).wait_send()
    for part in range(2 * T):
        for r in range(1, FS):
            l_copy(part, r).wait_send()
        for k in range(2 * NC - 1):
            r_copy(part, k).wait_send()

    @pl.when(s > 0)
    def _():
        for t in range(T):
            @pl.loop(0, CH)
            def _(c):
                for r in range(1, TP):
                    e_copy(t, r, c).wait_send()
                z_copy(t, c).wait_send()

    out.wait()


def solution(mesh):
    S, FS, TP = mesh.shape["section"], mesh.shape["fsdp"], mesh.shape["tp"]

    def per_device(stash, grad_now, grad_top, order, gain, weight):
        MB, n, D = stash.shape[1:]
        T = grad_top.shape[0]
        wl, N = weight.shape[1:]
        NC = FS // 2
        CH = D // pick(D, (384, 256, 128))
        WCH = 4 if wl % 64 == 0 else 1
        K = 2 * NC - 1
        DMA = pltpu.SemaphoreType.DMA
        V = pltpu.VMEM
        any_ = pl.BlockSpec(memory_space=pl.ANY)
        peers = max(TP - 1, 1)
        held, wg = pl.pallas_call(
            functools.partial(kernel, S, FS, TP, T),
            out_shape=(
                jax.ShapeDtypeStruct((1, n, D), bf16),
                jax.ShapeDtypeStruct((1, wl, N), bf16),
            ),
            in_specs=[
                pl.BlockSpec(memory_space=pltpu.SMEM),
                pl.BlockSpec(memory_space=pltpu.VMEM),
                any_, any_, any_, any_,
            ],
            out_specs=(any_, pl.BlockSpec(memory_space=pltpu.VMEM)),
            scratch_shapes=[
                V((FS * wl, N), bf16),
                V((MB, n, D), bf16),
                V(((T + 1) * n, D), bf16),
                V((T, n, D), bf16),
                V((T, n, 128), f32),
                V((T, n, D), bf16),
                V((2 * T, D, n), bf16),
                V((2 * T, wl, FS * n), bf16),
                V((2 * T, FS * n, N), bf16),
                V(((T + 1) * n, N), f32),
                V((T, n, N), f32),
                V((T, n, D), bf16),
                V((T, peers, n, D), bf16),
                V((T, n, D), bf16),
                V((wl, N), f32),
                DMA((3,)), DMA((T,)), DMA((2 * T,)), DMA((1,)),
                DMA((K, WCH)), DMA((K, WCH)),
                DMA((2 * T, FS - 1)), DMA((2 * T, FS - 1)),
                DMA((2 * T, K)), DMA((2 * T, K)),
                DMA((T, peers, CH)), DMA((T, peers, CH)),
                DMA((T, CH)), DMA((T, CH)),
            ],
            compiler_params=pltpu.CompilerParams(
                collective_id=0, has_side_effects=True, vmem_limit_bytes=60 * 1024 * 1024
            ),
        )(order, gain, stash, grad_now, grad_top, weight)
        return held, wg.astype(f32)

    return jax.shard_map(
        per_device,
        mesh=mesh,
        in_specs=(
            P("section", None, "fsdp", None),
            P("section", "fsdp", None),
            P(None, "fsdp", None),
            P("section", None),
            P("section", None),
            P("section", "fsdp", "tp"),
        ),
        out_specs=(P("section", "fsdp", None), P("section", "fsdp", "tp")),
        check_vma=False,
    )
```

time: 182 us -> 89.1 us (0.49)
  waiting for transfers between devices: 99.5 us -> 0 us
  Pallas kernels: 0 us -> 83.4 us
  blocking collectives: 24.8 us -> 0 us
  matrix products: 17.5 us -> 0 us
  between operations: 17.8 us -> 0.65 us
  other arithmetic: 12.6 us -> 3.02 us
  local copies, waits for them, and re-layouts: 6.68 us -> 0.82 us
  starting transfers between devices: 2.88 us -> 0 us
    pallas_call x0 -> x1, Pallas kernels: none -> 83.4 us  [per_device(): pl.pallas_call(functools.partial(kernel, S, FS, TP, T), out_shape=(jax.Sh...]
    all_gather x1 -> x0, waiting for transfers between devices: 32 us -> none  [per_device(): full_weight = lax.all_gather(weight[0], 'fsdp', axis=0, tiled=True)]
    reduce_scatter x1 -> x0, waiting for transfers between devices: 27.2 us -> none  [per_device(): lax.psum_scatter(lax.dot_general(lhs_all, rhs_all, (((0,), (0,)), ((), ()...]
    unnamed x6 -> x0, waiting for transfers between devices: 24.3 us -> none
    dot_general x5 -> x0, matrix products: 17.5 us -> none  [the longest x2 7.83 us: per_device(): products = jnp.dot(stacked, full_weight, preferred_element_type=jnp.float32)]
    ppermute x2 -> x0, waiting for transfers between devices: 16 us -> none  [shifted(): return lax.ppermute(shard, axis, pairs)]
    all_gather x2 -> x0, blocking collectives: 14.9 us -> none  [per_device(): grad_in = lax.all_gather(held_share, 'tp', axis=1, tiled=True)]
    psum x2 -> x0, blocking collectives: 9.85 us -> none  [per_device(): moment_sum = lax.psum(jnp.sum(gained * scaled_share, axis=-1), 'tp')]
  transfers between devices with their start and end apart: 6 -> 0, of which waited for: 6 -> 0; matrix products, arithmetic and copies ran while one was open for 8% -> 0% of each run, Pallas kernels for 0% -> 0%
where the time goes in v1:
time: 89.1 us; the launch traced here: 87.9 us
  Pallas kernels  83.4 us (94%)
  other arithmetic  3.02 us (3%)
    pallas_call x1, Pallas kernels, per_device(): pl.pallas_call(functools.partial(kernel, S, FS, TP, T), out_shape=(jax.Sh...  83.4 us
    convert_element_type x1, other arithmetic, per_device(): return (held, wg.astype(f32))  3.02 us

profile of v1, /device:TPU:0, one launch (start us, length us, event | category | flops | bytes accessed | tf_op | source)
XLA Modules:
  0.0 87.9 jit_solution(5222918828398635775)
XLA Ops:
  0.6 83.4 %shard_map.77 = (bf16[1,128,2304]{2,1,0:T(8,128)(2,1)}, bf16[1,576,1024]{2,1,0:T(8,128)(2,1)}) custom-call(s32[1,4]{1,0:T(1,128)} %order_ref.1, f32[1,2304]{1,0:T(1,128)} %gain_ref.1, bf16[1,4,128,2304]{3,2,1,0:T(8,128)(2,1)} %stash_ref.1, bf16[1,128,2304]{2,1,0:T(8,128)(2,1)} %gnow_ref.1, bf16[2,128,2304]{2,1,0:T(8,128)(2,1)} %gtop_ref.1, ...), custom_call_target="tpu_custom_call" | custom-call | tf_op jit(solution)/shard_map/pallas_call | solution.py:398
  84.0 0.0 copy-start
  84.0 3.0 %convert_element_type.3 = f32[1,576,1024]{2,1,0:T(8,128)} convert(bf16[1,576,1024]{2,1,0:T(8,128)(2,1)} %get-tuple-element.5) | non-fusion elementwise | flops 589824 | bytes 3538944 | tf_op jit(solution)/shard_map/convert_element_type | solution.py:437
  87.1 0.0 copy-done
  87.1 0.8 copy.9
Async XLA Ops:
  84.0 3.0 %copy-start = (bf16[1,128,2304]{2,1,0:T(8,128)(2,1)S(1)}, bf16[1,128,2304]{2,1,0:T(8,128)(2,1)}, u32[]{:S(2)}) copy-start(bf16[1,128,2304]{2,1,0:T(8,128)(2,1)} %get-tuple-element.8) | copy-start | bytes 1769476

commit v2 on v1

--- a/solution.py
+++ b/solution.py
@@ -36,7 +36,7 @@
     S, FS, TP, T, order_ref, gain_ref, stash_ref, gnow_ref, gtop_ref, w_ref,
     held_ref, wg_ref,
     wfull, stash, act, xt, inv, dyn, lt, lta, rhs, prod, slope, own_e, peer_e, dxs, acc,
-    lsem, topsem, ownsem, heldsem, w_s, w_r, l_s, l_r, r_s, r_r, e_s, e_r, z_s, z_r,
+    lsem, topsem, ownsem, heldsem, w_s, w_r, l_s, l_r, r_s, r_r, e_s, e_r, z_s, z_r, x_s, x_r,
 ):
     s = lax.axis_index("section")
     f = lax.axis_index("fsdp")
@@ -48,6 +48,8 @@
     n, D = act.shape[0] // (T + 1), act.shape[1]
     wl, N = w_ref.shape[1], w_ref.shape[2]
     WCH = w_s.shape[1]
+    wq = wl // TP
+    SPLIT = tuple(2 * t for t in range(T)) + (1,)
     wc = wl // WCH
     CW = D // e_s.shape[-1]
     CH = D // CW
@@ -98,12 +100,40 @@
         for j in range(WCH):
             w_copy(k, j).start()
 
-    def l_copy(part, r):
-        to = (f + r) % FS
-        return rcopy(
-            lt.at[part, pl.ds(to * wl, wl), :], lta.at[part, :, pl.ds(pl.multiple_of(f * n, n), n)],
-            l_s.at[part, r - 1], l_r.at[part, r - 1], {"fsdp": to},
-        )
+    def is_split(part):
+        return part in SPLIT and TP > 1
+
+    def l_copy(part, k):
+        cols = pl.ds(pl.multiple_of(f * n, n), n)
+        if k == 0:
+            to = sib
+        else:
+            o, cc = (k + 1) // 2, (k - 1) % 2
+            to = 2 * ((yc + o) % NC) + (core + cc) % 2
+        if k > 0 and is_split(part):
+            src = lt.at[part, pl.ds(to * wl + p * wq, wq), :]
+            dst = lta.at[part, pl.ds(p * wq, wq), cols]
+        else:
+            src = lt.at[part, pl.ds(to * wl, wl), :]
+            dst = lta.at[part, :, cols]
+        return rcopy(src, dst, l_s.at[part, k], l_r.at[part, k], {"fsdp": to})
+
+    def x_copy(part, k, q):
+        o, cc = (k + 1) // 2, (k - 1) % 2
+        src_f = 2 * ((yc - o + NC) % NC) + (core + cc) % 2
+        blk = lta.at[part, pl.ds(p * wq, wq), pl.ds(pl.multiple_of(src_f * n, n), n)]
+        return rcopy(blk, blk, x_s.at[part, k - 1, q - 1], x_r.at[part, k - 1, q - 1], {"tp": (p + q) % TP})
+
+    passed = set()
+
+    def l_pass(part):
+        if part in passed or not is_split(part):
+            return
+        passed.add(part)
+        for k in range(1, FS - 1):
+            l_copy(part, k).wait_recv()
+            for q in range(1, TP):
+                x_copy(part, k, q).start()
 
     def l_own(part):
         return pltpu.make_async_copy(
@@ -112,8 +142,8 @@
         )
 
     def l_send(part):
-        for r in range(1, FS):
-            l_copy(part, r).start()
+        for k in list(range(1, FS - 1)) + [0]:
+            l_copy(part, k).start()
         l_own(part).start()
 
     def r_copy(part, k):
@@ -253,78 +283,21 @@
         dxs[t, :, cols] = (dy.astype(f32) + total).astype(bf16)
         z_copy(t, c).start()
 
-    for t in range(T):
-        if t == 0:
-            gelu_rows(0, True)
-        r_ids = [0, 1] if t == 0 else [2 * t]
-
-        @pl.when(s > 0)
-        def _():
-            spread(t)
-
-        for part in r_ids:
-            r_send(part)
-        if t == 0:
-            for later in range(1, T):
-                gelu_rows(later, False)
-                r_send(2 * later + 1)
-
-        if t < T - 1:
-            @pl.when(s == S - 1)
-            def _():
-                pltpu.make_async_copy(gtop_ref.at[t], dyn.at[t], topsem.at[t]).wait()
-
-            gr = pl.ds(T * n, n)
-
-            @pl.loop(0, CH + LAG)
-            def _(i):
-                @pl.when((i < CH) & (s > 0))
-                def _():
-                    combine(t, i)
-
-                @pl.when(i >= LAG)
-                def _():
-                    c = i - LAG
-
-                    @pl.when(s < S - 1)
-                    def _():
-                        z_copy(t, c).wait_recv()
-
-                    cols = pl.ds(pl.multiple_of(c * CW, CW), CW)
-                    d = dyn[t, :, cols]
-                    lt[2 * t + 3, cols, :] = d.astype(f32).T.astype(bf16)
-                    g = jnp.dot(d, wfull[cols, :], preferred_element_type=f32)
-
-                    @pl.when(c == 0)
-                    def _():
-                        prod[gr, :] = g
-
-                    @pl.when(c > 0)
-                    def _():
-                        prod[gr, :] += g
-
-            l_send(2 * t + 3)
-
-            @pl.loop(0, n // rb)
-            def _(i):
-                rows = pl.ds(pl.multiple_of(i * rb, rb), rb)
-                g = prod[pl.ds(pl.multiple_of(T * n + i * rb, rb), rb), :]
-                here = pl.ds(pl.multiple_of(mine + i * rb, rb), rb)
-                rhs[2 * t + 2, here, :] = (slope[t + 1, rows, :] * g).astype(bf16)
-        else:
-            @pl.when(s > 0)
-            def _():
-                @pl.loop(0, CH)
-                def _(c):
-                    combine(t, c)
-
     parts = []
     for t in range(T):
         parts += [2 * t, 2 * t + 1] if t == 0 else [2 * t + 1, 2 * t]
-    for at, part in enumerate(parts):
+
+    def own_rows(at):
+        part = parts[at]
+        l_pass(part)
         l_own(part).wait()
-        for r in range(1, FS):
-            l_copy(part, r).wait_recv()
+        l_copy(part, 0).wait_recv()
+        for k in range(1, FS - 1):
+            if is_split(part):
+                for q in range(1, TP):
+                    x_copy(part, k, q).wait_recv()
+            else:
+                l_copy(part, k).wait_recv()
         for o in range(1, NC):
             r_copy(part, o).wait_recv()
             r_copy(part, NC - 1 + o).start()
@@ -344,6 +317,88 @@
             else:
                 acc[:, cols] = d
 
+    for t in range(T):
+        if t == 0:
+            gelu_rows(0, True)
+        r_ids = [0, 1] if t == 0 else [2 * t]
+
+        @pl.when(s > 0)
+        def _():
+            spread(t)
+
+        for part in r_ids:
+            r_send(part)
+        if t == 0:
+            for later in range(1, T):
+                gelu_rows(later, False)
+                r_send(2 * later + 1)
+
+        if t < T - 1:
+            @pl.when(s == S - 1)
+            def _():
+                pltpu.make_async_copy(gtop_ref.at[t], dyn.at[t], topsem.at[t]).wait()
+
+            gr = pl.ds(T * n, n)
+
+            @pl.loop(0, CH + LAG)
+            def _(i):
+                @pl.when((i < CH) & (s > 0))
+                def _():
+                    combine(t, i)
+
+                if t == 0:
+                    @pl.when(i == CH // 2)
+                    def _():
+                        l_pass(0)
+
+                    @pl.when(i == CH - 1)
+                    def _():
+                        l_pass(1)
+
+                @pl.when(i >= LAG)
+                def _():
+                    c = i - LAG
+
+                    @pl.when(s < S - 1)
+                    def _():
+                        z_copy(t, c).wait_recv()
+
+                    cols = pl.ds(pl.multiple_of(c * CW, CW), CW)
+                    d = dyn[t, :, cols]
+                    lt[2 * t + 3, cols, :] = d.astype(f32).T.astype(bf16)
+                    g = jnp.dot(d, wfull[cols, :], preferred_element_type=f32)
+
+                    @pl.when(c == 0)
+                    def _():
+                        prod[gr, :] = g
+
+                    @pl.when(c > 0)
+                    def _():
+                        prod[gr, :] += g
+
+            l_send(2 * t + 3)
+
+            @pl.loop(0, n // rb)
+            def _(i):
+                rows = pl.ds(pl.multiple_of(i * rb, rb), rb)
+                g = prod[pl.ds(pl.multiple_of(T * n + i * rb, rb), rb), :]
+                here = pl.ds(pl.multiple_of(mine + i * rb, rb), rb)
+                rhs[2 * t + 2, here, :] = (slope[t + 1, rows, :] * g).astype(bf16)
+        else:
+            for at in range(max(2 * T - 2, 0)):
+                own_rows(at)
+            for part in SPLIT:
+                l_pass(part)
+
+            @pl.when(s > 0)
+            def _():
+                @pl.loop(0, CH)
+                def _(c):
+                    combine(t, c)
+
+    for at in range(max(2 * T - 2, 0), 2 * T):
+        own_rows(at)
+
     t = T - 1
 
     @pl.when(s == S - 1)
@@ -363,8 +418,12 @@
         for k in range(2 * NC - 1):
             w_copy(k, j).wait_send()
     for part in range(2 * T):
-        for r in range(1, FS):
-            l_copy(part, r).wait_send()
+        for k in range(FS - 1):
+            l_copy(part, k).wait_send()
+        if is_split(part):
+            for k in range(1, FS - 1):
+                for q in range(1, TP):
+                    x_copy(part, k, q).wait_send()
         for k in range(2 * NC - 1):
             r_copy(part, k).wait_send()
 
@@ -429,6 +488,7 @@
                 DMA((2 * T, K)), DMA((2 * T, K)),
                 DMA((T, peers, CH)), DMA((T, peers, CH)),
                 DMA((T, CH)), DMA((T, CH)),
+                DMA((2 * T, max(FS - 2, 1), peers)), DMA((2 * T, max(FS - 2, 1), peers)),
             ],
             compiler_params=pltpu.CompilerParams(
                 collective_id=0, has_side_effects=True, vmem_limit_bytes=60 * 1024 * 1024

time: 89.1 us -> 85.8 us (0.963); the launches traced: 87.9 us -> 85.6 us
  Pallas kernels: 83.4 us -> 81.1 us
    pallas_call x1, Pallas kernels: 83.4 us -> 81.1 us  [per_device(): pl.pallas_call(functools.partial(kernel, S, FS, TP, T), out_shape=(jax.Sh...]
where the time goes in v2:
time: 85.8 us; the launch traced here: 85.6 us
  Pallas kernels  81.1 us (95%)
  other arithmetic  3.02 us (4%)
    pallas_call x1, Pallas kernels, per_device(): pl.pallas_call(functools.partial(kernel, S, FS, TP, T), out_shape=(jax.Sh...  81.1 us
    convert_element_type x1, other arithmetic, per_device(): return (held, wg.astype(f32))  3.02 us

profile of v2, /device:TPU:0, one launch (start us, length us, event | category | flops | bytes accessed | tf_op | source)
XLA Modules:
  0.0 85.6 jit_solution(13358794173078146086)
XLA Ops:
  0.6 81.1 %shard_map.77 = (bf16[1,128,2304]{2,1,0:T(8,128)(2,1)}, bf16[1,576,1024]{2,1,0:T(8,128)(2,1)}) custom-call(s32[1,4]{1,0:T(1,128)} %order_ref.1, f32[1,2304]{1,0:T(1,128)} %gain_ref.1, bf16[1,4,128,2304]{3,2,1,0:T(8,128)(2,1)} %stash_ref.1, bf16[1,128,2304]{2,1,0:T(8,128)(2,1)} %gnow_ref.1, bf16[2,128,2304]{2,1,0:T(8,128)(2,1)} %gtop_ref.1, ...), custom_call_target="tpu_custom_call" | custom-call | tf_op jit(solution)/shard_map/pallas_call | solution.py:457
  81.7 0.0 copy-start
  81.7 3.0 %convert_element_type.3 = f32[1,576,1024]{2,1,0:T(8,128)} convert(bf16[1,576,1024]{2,1,0:T(8,128)(2,1)} %get-tuple-element.5) | non-fusion elementwise | flops 589824 | bytes 3538944 | tf_op jit(solution)/shard_map/convert_element_type | solution.py:497
  84.8 0.0 copy-done
  84.8 0.8 copy.9
Async XLA Ops:
  81.7 3.0 %copy-start = (bf16[1,128,2304]{2,1,0:T(8,128)(2,1)S(1)}, bf16[1,128,2304]{2,1,0:T(8,128)(2,1)}, u32[]{:S(2)}) copy-start(bf16[1,128,2304]{2,1,0:T(8,128)(2,1)} %get-tuple-element.8) | copy-start | bytes 1769476
